TPU v7x, 32 devices: a whole 2x2x4 slice. The times are simulated.
32 devices in a mesh: layer: 4 (over y, core), row: 4 (over z), col: 2 (over x).
Axes of the slice: x: 2, y: 2, z: 4, core: 2. Of those that a mesh axis runs over, the one named last changes fastest.
Arguments:
- left: float32 [2048, 1024], P('row', ('layer', 'col')), may hold values from -6 to 6
- right: float32 [1024, 32768], P(('layer', 'row'), 'col'), may hold values from -0.1875 to 0.1875
Outputs:
- product: float32 [2048, 32768], P(('row', 'layer'), 'col')
All inputs are finite; a program needn't handle non-finite values.
Results may differ from a plain program's by a relative error of at most 0.000076.
Values sent between devices are 32-bit elements; how exact they have to be, the bound alone decides.
A program may use at most 128 MiB of HBM per device.

v0:
```python
import jax
import jax.numpy as jnp
from jax import lax
from jax.sharding import PartitionSpec as P


def body(left, right):
    panel = lax.all_gather(left, "col", axis=1, tiled=True)
    full_rows = lax.all_to_all(panel, "layer", split_axis=0, concat_axis=1, tiled=True)
    operand = lax.all_gather(right, ("layer", "row"), axis=0, tiled=True)
    return jnp.dot(
        full_rows, operand, precision=lax.Precision.HIGHEST, preferred_element_type=jnp.float32
    )


def solution(mesh):
    in_specs = (P("row", ("layer", "col")), P(("layer", "row"), "col"))
    out_specs = P(("row", "layer"), "col")
    return jax.shard_map(body, mesh=mesh, in_specs=in_specs, out_specs=out_specs, check_vma=False)
```

profile of v0, /device:TPU:1, one launch (start us, length us, event | category | flops | bytes accessed | tf_op | source)
XLA Modules:
  0.0 412.3 jit_solution(14619808681469267005)
XLA Ops:
  6.5 0.0 all-gather.2.cloned.1.call-start
  6.5 0.7 all-gather.2.cloned.1.call-update
  7.3 9.0 %all_gather.6 = f32[512,256]{1,0:T(8,128)S(1)} all-gather(f32[512,128]{1,0:T(8,128)} %param.2), channel_id=1, replica_groups=mesh['layer'=4,'row'=4,'col'=2] {'col'}, dimensions={1}, use_global_device_ids=true | all-gather | bytes 786432 | tf_op jit(solution)/shard_map/all_gather | solution.py:8
  16.2 15.2 %all_to_all.19 = f32[4,128,256]{2,1,0:T(8,128)S(1)} all-to-all(f32[4,128,256]{2,1,0:T(8,128)S(1)} %bitcast.7), channel_id=1, replica_groups=mesh['layer'=4,'row'=4,'col'=2] {'layer'}, dimensions={0} | all-to-all | bytes 1048576 | tf_op jit(solution)/shard_map/all_to_all | solution.py:9
  31.4 0.2 copy.3
  31.6 331.9 %all-gather.2.cloned.1.call-done = f32[1024,16384]{1,0:T(8,128)} async-done(((f32[64,16384]{1,0:T(8,128)}), f32[1024,16384]{1,0:T(8,128)}) %all-gather.2.cloned.1.call-update) | async-done | bytes 67108880 | tf_op jit(solution)/shard_map/all_gather | solution.py:10
  363.5 42.0 %fusion = f32[128,16384]{1,0:T(8,128)} fusion(f32[128,1024]{0,1:T(8,128)S(1)} %bitcast.5, f32[1024,16384]{1,0:T(8,128)} %all-gather.2.cloned.1.call-done), kind=kOutput, calls=%fused_computation | convolution fusion | flops 25769803776 | bytes 76021760 | tf_op jit(solution)/shard_map/dot_general | solution.py:11
Async XLA Ops:
  6.5 356.9 %all-gather.2.cloned.1.call-start = ((), (), s32[]{:S(2)}) async-start(), calls=%async_computation.1 | async-start | bytes 71303168 | tf_op jit(solution)/shard_map/all_gather | solution.py:10
Sparse Core Ops, SparseCore 0:
  8.9 354.5 all-gather.1
where the time goes:
time: 412 us
  waiting for transfers between devices  333 us (81%)
  matrix products  42 us (10%)
  blocking collectives  24.1 us (6%)
  between operations  13.4 us (3%)
    all_gather x1, waiting for transfers between devices, body(): operand = lax.all_gather(right, ('layer', 'row'), axis=0, tiled=True)  332 us
    dot_general x1, matrix products, body(): jnp.dot(full_rows, operand, precision=lax.Precision.HIGHEST, preferred_el...  42 us
    all_to_all x1, blocking collectives, body(): lax.all_to_all(panel, 'layer', split_axis=0, concat_axis=1, tiled=True)  15.2 us
    all_gather x1, blocking collectives, body(): panel = lax.all_gather(left, 'col', axis=1, tiled=True)  8.97 us
  transfers between devices with their start and end apart: 1, of which 1 were waited for; matrix products, arithmetic and copies ran while one was open for 0% of the time, Pallas kernels for 0%

commit v1 on v0

v1 whole, which is shorter than its diff:
```python
import functools

import jax
import jax.numpy as jnp
from jax import lax
from jax.experimental import pallas as pl
from jax.experimental.pallas import tpu as pltpu
from jax.sharding import PartitionSpec as P

MESH = pl.DeviceIdType.MESH
CORES = 2
AHEAD = 3
LEAD = 2
LEAD_OUTER = 6


def kernel(sizes, left, right, out, a_f32, a_hi, a_lo, b_all, b_hi, b_lo, c_buf,
           a1_s, a1_r, a2_s, a2_r, a3_s, a3_r, b1_s, b1_r, b2_s, b2_r, c_s, c_r, d_s, d_r):
    layers, rows, cols, chunks, width, tile = sizes
    half = rows // 2
    chips = layers // CORES
    l, z = lax.axis_index("layer"), lax.axis_index("row")
    x = lax.axis_index("col") if cols > 1 else 0
    y, c = l // CORES, l % CORES
    side = z // half
    base = side * half
    centre = half - 1 + side
    own = z - base
    piece = l * cols + x
    block = c_buf.shape[2] // layers
    is_centre = z == centre
    sibling = y * CORES + (1 - c)

    def remote(src, dst, send, recv, **to):
        return pltpu.make_async_remote_copy(
            src_ref=src, dst_ref=dst, send_sem=send, recv_sem=recv, device_id=to, device_id_type=MESH)

    barrier = pltpu.get_barrier_semaphore()
    greeted = 0
    for k in range(1, layers):
        pl.semaphore_signal(barrier, inc=1, device_id={"layer": lax.rem(l + k, layers)}, device_id_type=MESH)
        greeted += 1
    for k in range(1, rows):
        pl.semaphore_signal(barrier, inc=1, device_id={"row": lax.rem(z + k, rows)}, device_id_type=MESH)
        greeted += 1
    for k in range(1, cols):
        for m in range(chips):
            to = {"layer": lax.rem(l + m * CORES, layers), "col": lax.rem(x + k, cols)}
            pl.semaphore_signal(barrier, inc=1, device_id=to, device_id_type=MESH)
            greeted += 1
    pl.semaphore_wait(barrier, greeted)

    def b1(j, k):
        q = lax.rem(l + k, layers)
        src = right.at[:, pl.ds(pl.multiple_of((q * chunks + j) * width, width), width)]
        if k == 0:
            return pltpu.make_async_copy(src, b_all.at[j, l, z], b1_r.at[j, 0])
        return remote(src, b_all.at[j, l, z], b1_s.at[j, k], b1_r.at[j, k], layer=q)

    def b1_start(j):
        for k in range(layers):
            b1(j, k).start()

    def b1_wait(j):
        b1(j, 0).wait()
        for k in range(1, layers):
            b1(j, k).wait_recv()

    def b2(j, t):
        to = half - 1 + t
        return remote(b_all.at[j, :, z], b_all.at[j, :, z], b2_s.at[j, t], b2_r.at[j, z], row=to)

    def b2_start(j):
        for t in range(2):
            @pl.when(z != half - 1 + t)
            def _():
                b2(j, t).start()

    def b2_wait(j):
        for k in range(1, rows):
            src = lax.rem(z + k, rows)
            remote(b_all.at[j, :, src], b_all.at[j, :, src], b2_s.at[j, 0], b2_r.at[j, src], row=src).wait_recv()

    def gather_step(j):
        @pl.when(j + AHEAD < chunks)
        def _():
            b1_start(j + AHEAD)
        b1_wait(j)
        b2_start(j)

    def c_copy(j, s):
        return remote(c_buf.at[j, s], c_buf.at[j, s], c_s.at[j, s], c_r.at[j], row=base + s)

    def dist(j, k):
        q = lax.rem(l + k, layers)
        src = c_buf.at[j, own, pl.ds(pl.multiple_of(q * block, block), block)]
        dst = out.at[:, pl.ds(pl.multiple_of((l * chunks + j) * width, width), width)]
        if k == 0:
            return pltpu.make_async_copy(src, dst, d_r.at[j, 0])
        return remote(src, dst, d_s.at[j, k], d_r.at[j, k], layer=q)

    def dist_start(j):
        for k in range(1, layers):
            dist(j, k).start()
        dist(j, 0).start()

    def a1(s):
        return remote(left, a_f32.at[s, piece], a1_s, a1_r.at[s], row=centre)

    def a2(s, m, k, src):
        to = {"layer": lax.rem(l + m * CORES, layers)}
        if cols > 1:
            to["col"] = lax.rem(x + k, cols)
        return remote(src, a_f32.at[s, piece], a2_s.at[s, m, k], a2_r.at[s, m, k], **to)

    peers = [(m, k) for m in range(chips) for k in range(cols) if (m, k) != (0, 0)]

    def a3(s, m, k, core):
        ls = lax.rem(y + chips - m, chips) * CORES + core
        xs = lax.rem(x + cols - k, cols)
        p = ls * cols + xs
        return remote(a_f32.at[s, p], a_f32.at[s, p], a3_s.at[s, m, k], a3_r.at[s, m, k], layer=sibling)

    def local_a():
        return pltpu.make_async_copy(left, a_f32.at[own, piece], a1_r.at[own])

    def product(j):
        b = b_all[j].reshape(b_hi.shape)
        hi = b.astype(jnp.bfloat16)
        b_hi[...] = hi
        b_lo[...] = (b - hi.astype(jnp.float32)).astype(jnp.bfloat16)
        per = c_buf.shape[2] // tile
        for s in range(half):
            @pl.loop(0, per)
            def _(t):
                at = pl.ds(pl.multiple_of(t * tile, tile), tile)
                ah, al = a_hi[s, at, :], a_lo[s, at, :]
                dot = functools.partial(jnp.dot, preferred_element_type=jnp.float32)
                c_buf[j, s, at, :] = dot(al, b_hi[...]) + dot(ah, b_lo[...]) + dot(ah, b_hi[...])

    for j in range(min(AHEAD, chunks)):
        b1_start(j)
        if j == 0:
            @pl.when(jnp.logical_not(is_centre))
            def _():
                a1(own).start()

            @pl.when(is_centre)
            def _():
                local_a().start()
                for m, k in peers:
                    a2(own, m, k, left).start()

    lead = min(LEAD, chunks)
    lead_outer = min(LEAD_OUTER, chunks)

    @pl.when(is_centre)
    def _():
        @pl.loop(0, lead)
        def _(j):
            gather_step(j)
        local_a().wait()
        for i in range(1, half):
            s = lax.rem(own + i, half)
            a1(s).wait_recv()
            for m, k in peers:
                a2(s, m, k, a_f32.at[s, piece]).start()
        for i in range(half):
            s = lax.rem(own + i, half)
            a3(s, 0, 0, c).start()
            for m, k in peers:
                a2(s, m, k, left).wait_recv()
                a3(s, m, k, c).start()
        for i in range(half):
            s = lax.rem(own + i, half)
            for m, k in [(0, 0)] + peers:
                a3(s, m, k, 1 - c).wait_recv()
        wide = a_f32.shape[3]
        for s in range(half):
            for p in range(layers * cols):
                a = a_f32[s, p]
                hi = a.astype(jnp.bfloat16)
                a_hi[s, :, p * wide:(p + 1) * wide] = hi
                a_lo[s, :, p * wide:(p + 1) * wide] = (a - hi.astype(jnp.float32)).astype(jnp.bfloat16)

        @pl.loop(0, chunks)
        def _(j):
            @pl.when(j + lead < chunks)
            def _():
                gather_step(j + lead)
            b2_wait(j)
            product(j)
            for i in range(1, half):
                c_copy(j, lax.rem(own + i, half)).start()
            dist_start(j)

    @pl.when(jnp.logical_not(is_centre))
    def _():
        @pl.loop(0, lead_outer)
        def _(j):
            gather_step(j)

        @pl.loop(0, chunks)
        def _(j):
            @pl.when(j + lead_outer < chunks)
            def _():
                gather_step(j + lead_outer)
            c_copy(j, own).wait_recv()
            dist_start(j)

    @pl.loop(0, chunks)
    def _(j):
        dist(j, 0).wait()
        for k in range(1, layers):
            dist(j, k).wait()
            b1(j, k).wait_send()
        for t in range(2):
            @pl.when(z != half - 1 + t)
            def _():
                b2(j, t).wait_send()

        @pl.when(is_centre)
        def _():
            for i in range(1, half):
                c_copy(j, lax.rem(own + i, half)).wait_send()

    @pl.when(jnp.logical_not(is_centre))
    def _():
        a1(own).wait_send()

    @pl.when(is_centre)
    def _():
        for i in range(half):
            s = lax.rem(own + i, half)
            for m, k in peers:
                a2(s, m, k, left).wait_send()
            for m, k in [(0, 0)] + peers:
                a3(s, m, k, c).wait_send()


def body(mesh, left, right):
    layers, rows, cols = mesh.shape["layer"], mesh.shape["row"], mesh.shape["col"]
    if left.shape[1] % 128:
        left = lax.all_gather(left, "col", axis=1, tiled=True)
        cols = 1
    height, wide = left.shape
    depth, across = right.shape
    share = across // layers
    width = max(128, share // 16)
    chunks = share // width
    half = rows // 2
    inner = depth * layers * rows
    dma = pltpu.SemaphoreType.DMA
    sizes = (layers, rows, cols, chunks, width, min(256, height))
    chips = layers // CORES
    f32, bf16 = jnp.float32, jnp.bfloat16
    return pl.pallas_call(
        functools.partial(kernel, sizes),
        out_shape=jax.ShapeDtypeStruct((height // layers, across), f32),
        in_specs=[pl.BlockSpec(memory_space=pl.ANY)] * 2,
        out_specs=pl.BlockSpec(memory_space=pl.ANY),
        scratch_shapes=[
            pltpu.VMEM((half, layers * cols, height, wide), f32),
            pltpu.VMEM((half, height, inner), bf16),
            pltpu.VMEM((half, height, inner), bf16),
            pltpu.VMEM((chunks, layers, rows, depth, width), f32),
            pltpu.VMEM((inner, width), bf16),
            pltpu.VMEM((inner, width), bf16),
            pltpu.VMEM((chunks, half, height, width), f32),
            dma, dma((half,)),
            dma((half, chips, cols)), dma((half, chips, cols)),
            dma((half, chips, cols)), dma((half, chips, cols)),
            dma((chunks, layers)), dma((chunks, layers)),
            dma((chunks, 2)), dma((chunks, rows)),
            dma((chunks, half)), dma((chunks,)),
            dma((chunks, layers)), dma((chunks, layers)),
        ],
        compiler_params=pltpu.CompilerParams(
            collective_id=1, has_side_effects=True, vmem_limit_bytes=60 * 2**20),
    )(left, right)


def solution(mesh):
    in_specs = (P("row", ("layer", "col")), P(("layer", "row"), "col"))
    out_specs = P(("row", "layer"), "col")
    return jax.shard_map(
        functools.partial(body, mesh), mesh=mesh, in_specs=in_specs, out_specs=out_specs, check_vma=False)
```

time: 412 us -> 248 us (0.60)
  waiting for transfers between devices: 333 us -> 0 us
  Pallas kernels: 0 us -> 240 us
  matrix products: 42 us -> 0 us
  blocking collectives: 24.1 us -> 0 us
  between operations: 13.4 us -> 0.01 us
  local copies, waits for them, and re-layouts: 0.19 us -> 7.59 us
    all_gather x1 -> x0, waiting for transfers between devices: 332 us -> none  [body(): operand = lax.all_gather(right, ('layer', 'row'), axis=0, tiled=True)]
    pallas_call x0 -> x1, Pallas kernels: none -> 240 us  [body(): pl.pallas_call(functools.partial(kernel, sizes), out_shape=jax.ShapeDtype...]
    dot_general x1 -> x0, matrix products: 42 us -> none  [body(): jnp.dot(full_rows, operand, precision=lax.Precision.HIGHEST, preferred_el...]
    all_to_all x1 -> x0, blocking collectives: 15.2 us -> none  [body(): lax.all_to_all(panel, 'layer', split_axis=0, concat_axis=1, tiled=True)]
    all_gather x1 -> x0, blocking collectives: 8.97 us -> none  [body(): panel = lax.all_gather(left, 'col', axis=1, tiled=True)]
    unnamed x0 -> x1, local copies, waits for them, and re-layouts: none -> 7.59 us
  transfers between devices with their start and end apart: 1 -> 0, of which waited for: 1 -> 0; matrix products, arithmetic and copies ran while one was open for 0% -> 0% of each run, Pallas kernels for 0% -> 0%
where the time goes in v1:
time: 248 us; the launch traced here: 247 us
  Pallas kernels  240 us (97%)
  local copies, waits for them, and re-layouts  7.59 us (3%)
    pallas_call x1, Pallas kernels, body(): pl.pallas_call(functools.partial(kernel, sizes), out_shape=jax.ShapeDtype...  240 us
    unnamed x1, local copies, waits for them, and re-layouts  7.59 us

profile of v1, /device:TPU:1, one launch (start us, length us, event | category | flops | bytes accessed | tf_op | source)
XLA Modules:
  0.0 247.4 jit_solution(17577745168237550502)
XLA Ops:
  0.0 239.8 %shard_map.28 = f32[128,16384]{1,0:T(8,128)} custom-call(f32[512,128]{1,0:T(8,128)} %left.1, f32[64,16384]{1,0:T(8,128)} %right.1), custom_call_target="tpu_custom_call" | custom-call | tf_op jit(solution)/shard_map/pallas_call | solution.py:257
  239.8 7.6 %copy.4 = f32[128,16384]{1,0:T(8,128)} copy(f32[128,16384]{1,0:T(8,128)} %shard_map.28) | data formatting | bytes 16777216
